TPU v7x, 256 devices: a whole 4x4x8 slice. The times are simulated.
256 devices in a mesh: ctx: 32 (over z_lo, x, core), exp: 8 (over z_hi, y).
Axes of the slice: x: 4, y: 4, z: 8 (z_hi: 2, z_lo: 4; z = z_hi * 4 + z_lo), core: 2. Of those that a mesh axis runs over, the one named last changes fastest.
Arguments:
- hidden_in: bfloat16 [4096, 4096], P('ctx', 'exp'), may hold values from -6 to 6
- query_vectors: bfloat16 [4096, 2048], P('ctx', 'exp'), may hold values from -6 to 6
- key_vectors: bfloat16 [4096, 2048], P('ctx', 'exp'), may hold values from -6 to 6
- value_vectors: bfloat16 [4096, 2048], P('ctx', 'exp'), may hold values from -24 to 24
- out_weight: bfloat16 [2048, 4096], P('exp'), may hold values from -0.125 to 0.125
- norm_gain: float32 [4096], replicated, may hold values from 0.5 to 1.5
- gate_proj: bfloat16 [8, 4096, 11008], P('exp', None, 'ctx'), may hold values from -0.09375 to 0.09375
- up_proj: bfloat16 [8, 4096, 11008], P('exp', None, 'ctx'), may hold values from -0.09375 to 0.09375
- down_proj: bfloat16 [8, 11008, 4096], P('exp', 'ctx'), may hold values from -0.0546875 to 0.0546875
- expert_ids: int32 [4096, 2], P('ctx'), may hold values from 0 to 7, all different within a row; in each aligned block of 128 rows (0 to 127, 128 to 255, ...) at most 40 rows name the same one
- gate_scale: float32 [4096, 2], P('ctx'), may hold values from 0.1 to 1
Outputs:
- layer_out: bfloat16 [4096, 4096], P('ctx', 'exp')
Inputs may be any that keep to these rules, and one draw needn't show every extreme that they name: `expert_ids`: each row names two different experts. In each aligned block of 128 rows (the rows of one ctx device) no expert is named by more than 40 rows, and in some blocks some expert is named by exactly 40 rows.
All inputs are finite; a program needn't handle non-finite values.
Results may differ from a plain program's by a relative error of at most 0.017.
Values may be sent and summed in bfloat16 or wider, within the bound.
No kernel may reach another device: no remote copies, remote signals or barrier semaphores. Data moves between devices by JAX's collectives and lax.ppermute only.
A program may use at most 128 MiB of HBM per device.

v0:
```python
import jax
import jax.numpy as jnp
from jax import lax
from jax.sharding import PartitionSpec as P

HEAD_DIM = 128


epsilon = 1e-05
masked_score = -1e30


def sent_together(arrays, axis, dim, along):
    widths = [a.shape[along] for a in arrays]
    both = jnp.concatenate(arrays, axis=along)
    filled = lax.all_gather(both, axis, axis=dim, tiled=True)
    return tuple(jnp.split(filled, [sum(widths[:k]) for k in range(1, len(widths))], axis=along))


def in_blocks(x, dim, devices):
    dims = x.shape
    pieces = x.reshape(*dims[:dim], devices, dims[dim] // devices, *dims[dim + 1 :])
    return jnp.moveaxis(pieces, dim, 0)


def summed_on_arrival(x, axis, dim):
    pieces = in_blocks(x, dim, lax.axis_size(axis))
    arrived = lax.all_to_all(pieces, axis, split_axis=0, concat_axis=0, tiled=True)
    return arrived.astype(jnp.float32).sum(axis=0)


def attend(carried, query_heads, key_rows, value_rows, query_offset, needed):
    running_max, running_sum, weighted = carried
    head_count, row_count, head_width = query_heads.shape
    key_count = key_rows.shape[0]
    key_split = key_rows.reshape(key_count, head_count, head_width)
    value_split = value_rows.reshape(key_count, head_count, head_width)
    scores = jnp.einsum(
        "hqd,khd->hqk", query_heads, key_split, preferred_element_type=jnp.float32
    ) * HEAD_DIM ** (-0.5)
    query_pos = query_offset + lax.broadcasted_iota(jnp.int32, (row_count, key_count), 0)
    key_pos = lax.broadcasted_iota(jnp.int32, (row_count, key_count), 1)
    visible = jnp.logical_and(key_pos <= query_pos, needed)
    scores = jnp.where(visible[None], scores, masked_score)
    new_max = jnp.maximum(running_max, jnp.max(scores, axis=2))
    weights = jnp.where(visible[None], jnp.exp(scores - new_max[..., None]), 0.0)
    running_sum = jnp.sum(weights, axis=2)
    weighted = jnp.einsum(
        "hqk,khd->hqd",
        weights.astype(jnp.bfloat16),
        value_split,
        preferred_element_type=jnp.float32,
    )
    return (new_max, running_sum, weighted)


def fold_block(carried, query_heads, key_rows, value_rows, query_offset, needed):
    needed = jnp.asarray(needed)
    return attend(carried, query_heads, key_rows, value_rows, query_offset, needed)


def local(
    hidden_in,
    query_vectors,
    key_vectors,
    value_vectors,
    out_weight,
    norm_gain,
    gate_proj,
    up_proj,
    down_proj,
    expert_ids,
    gate_scale,
):
    row_count, local_width = hidden_in.shape
    head_count = query_vectors.shape[1] // HEAD_DIM
    ctx_index = lax.axis_index("ctx")
    my_offset = ctx_index * row_count
    query_heads = query_vectors.reshape(row_count, head_count, HEAD_DIM).transpose(1, 0, 2)
    initial = (
        jnp.full((head_count, row_count), masked_score, jnp.float32),
        jnp.zeros((head_count, row_count), jnp.float32),
        jnp.zeros((head_count, row_count, HEAD_DIM), jnp.float32),
    )
    pieces = sent_together((key_vectors, value_vectors), "ctx", 0, 1)
    carried = fold_block(initial, query_heads, pieces[0], pieces[1], my_offset, True)
    running_max, running_sum, weighted = carried
    attended = (
        (weighted / running_sum[..., None])
        .transpose(1, 0, 2)
        .reshape(row_count, head_count * HEAD_DIM)
        .astype(jnp.bfloat16)
    )
    projected = summed_on_arrival(
        lax.dot_general(
            out_weight, attended, (((0,), (1,)), ((), ())), preferred_element_type=jnp.float32
        ).astype(jnp.bfloat16),
        "exp",
        0,
    ).T
    residual = (hidden_in.astype(jnp.float32) + projected).astype(jnp.bfloat16)
    residual_wide = residual.astype(jnp.float32)
    expert_count = lax.axis_size("exp")
    capacity = min(row_count, 5 * row_count // (2 * expert_count))
    flat_ids = expert_ids.reshape(row_count * 2)
    onehot = (
        flat_ids[:, None] == lax.broadcasted_iota(jnp.int32, (row_count * 2, expert_count), 1)
    ).astype(jnp.int32)
    earlier = jnp.cumsum(onehot, axis=0) - onehot
    slot_index = jnp.sum(earlier * onehot, axis=1)
    target = flat_ids * capacity + slot_index
    placing = (
        target[None, :]
        == lax.broadcasted_iota(jnp.int32, (expert_count * capacity, row_count * 2), 0)
    ).astype(jnp.bfloat16)
    placing_tokens = jnp.sum(placing.reshape(expert_count * capacity, row_count, 2), axis=2)
    buffer = jnp.dot(placing_tokens, residual, preferred_element_type=jnp.float32).astype(
        jnp.bfloat16
    )
    arrived = lax.all_to_all(buffer, "exp", split_axis=0, concat_axis=1, tiled=True)
    arrived_wide = arrived.astype(jnp.float32)
    inverse = lax.rsqrt(jnp.mean(arrived_wide * arrived_wide, axis=1, keepdims=True) + epsilon)
    arrived = (arrived_wide * inverse * norm_gain[None, :]).astype(jnp.bfloat16)
    w_gate = gate_proj[0]
    w_up = up_proj[0]
    w_down = down_proj[0]
    piece_rows = lax.all_gather(arrived, "ctx", axis=0, tiled=True)
    gate_act = jnp.dot(piece_rows, w_gate, preferred_element_type=jnp.float32)
    up_act = jnp.dot(piece_rows, w_up, preferred_element_type=jnp.float32)
    hidden = (jax.nn.silu(gate_act) * up_act).astype(jnp.bfloat16)
    result = lax.psum_scatter(
        jnp.dot(hidden, w_down, preferred_element_type=jnp.float32).astype(jnp.bfloat16),
        "ctx",
        scatter_dimension=0,
        tiled=True,
    )
    returned = lax.all_to_all(result, "exp", split_axis=1, concat_axis=0, tiled=True)
    gathered_back = lax.dot_general(
        placing, returned, (((0,), (0,)), ((), ())), preferred_element_type=jnp.float32
    )
    gathered_back = gathered_back.reshape(row_count, 2, local_width)
    combined = (
        residual_wide
        + gate_scale[:, 0:1] * gathered_back[:, 0]
        + gate_scale[:, 1:2] * gathered_back[:, 1]
    )
    return combined.astype(jnp.bfloat16)


def solution(mesh):
    placed = (
        P("ctx", "exp"),
        P("ctx", "exp"),
        P("ctx", "exp"),
        P("ctx", "exp"),
        P("exp", None),
        P(),
        P("exp", None, "ctx"),
        P("exp", None, "ctx"),
        P("exp", "ctx", None),
        P("ctx", None),
        P("ctx", None),
    )
    return jax.shard_map(
        local, mesh=mesh, in_specs=placed, out_specs=P("ctx", "exp"), check_vma=False
    )
```

profile of v0, /device:TPU:8, one launch (start us, length us, event | category | flops | bytes accessed | tf_op | source)
XLA Modules:
  0.0 434.5 jit_solution(4455105996812060525)
XLA Ops:
  6.5 1.1 copy.56
  7.6 1.0 copy.57
  8.6 0.7 pad_maximum_fusion
  9.3 0.3 iota_compare_fusion
  9.7 72.9 %all-gather.3.cloned.1.call-done = bf16[4096,512]{0,1:T(8,128)(2,1)} async-done(((bf16[128,512]{0,1:T(8,128)(2,1)}), bf16[4096,512]{0,1:T(8,128)(2,1)}) %all-gather.3.cloned.1.call-update) | async-done | bytes 4194320 | tf_op jit(solution)/shard_map/all_gather | solution.py:16
  82.6 2.7 fusion.53
  85.3 1.3 fusion.54
  86.7 0.8 fusion.2
  87.5 1.4 fusion.29
  89.0 0.1 copy-done.1
  89.1 0.5 convolution_convert_fusion.1
  89.6 1.1 copy.81
  90.8 9.0 %all-to-all-start = ((bf16[8,512,128]{1,2,0:T(8,128)(2,1)}), bf16[8,512,128]{1,2,0:T(8,128)(2,1)}, u32[]{:S(2)}, u32[]{:S(2)}) async-start(bf16[8,512,128]{1,2,0:T(8,128)(2,1)} %bitcast.108), calls=%async_computation | async-start | bytes 2097152 | tf_op jit(solution)/shard_map/all_to_all | solution.py:28
  100.0 0.1 reshape.105
  100.2 0.6 reduce-window.6
  100.8 0.2 slice_reduce_fusion
  101.4 18.2 %all-to-all-done = bf16[8,512,128]{1,2,0:T(8,128)(2,1)} async-done(((bf16[8,512,128]{1,2,0:T(8,128)(2,1)}), bf16[8,512,128]{1,2,0:T(8,128)(2,1)}, u32[]{:S(2)}, u32[]{:S(2)}) %all-to-all-start) | async-done | bytes 1048608 | tf_op jit(solution)/shard_map/all_to_all | solution.py:28
  119.6 1.4 convert_reduce_fusion
  121.0 0.2 convolution_convert_fusion.2
  121.3 22.9 %all_to_all.37 = bf16[8,40,512]{2,1,0:T(8,128)(2,1)S(1)} all-to-all(bf16[8,40,512]{2,1,0:T(8,128)(2,1)S(1)} %bitcast.111), channel_id=1, replica_groups=mesh['ctx'=32,'exp'=8] {'exp'}, dimensions={0} | all-to-all | bytes 655360 | tf_op jit(solution)/shard_map/all_to_all | solution.py:120
  144.3 0.2 fusion.33
  144.5 0.9 multiply_convert_fusion
  145.4 0.2 reduce-scatter.2.cloned.1.call-start
  145.6 70.3 %all-gather.5.cloned.1.call-done = bf16[1280,4096]{1,0:T(8,128)(2,1)} async-done(((bf16[40,4096]{1,0:T(8,128)(2,1)}), bf16[1280,4096]{1,0:T(8,128)(2,1)}) %all-gather.5.cloned.1.call-update) | async-done | bytes 10485776 | tf_op jit(solution)/shard_map/all_gather | solution.py:127
  215.9 9.9 %fusion.6 = f32[1280,344]{0,1:T(8,128)} fusion(bf16[1280,4096]{1,0:T(8,128)(2,1)} %all-gather.5.cloned.1.call-done, bf16[1,4096,344]{1,2,0:T(8,128)(2,1)} %param.17), kind=kOutput, calls=%fused_computation.11 | convolution fusion | flops 3607101440 | bytes 15065088 | tf_op jit(solution)/shard_map/dot_general | solution.py:128
  225.7 19.3 %convolution_convert_fusion = bf16[1280,4096]{1,0:T(8,128)(2,1)} fusion(bf16[1,344,4096]{2,1,0:T(8,128)(2,1)S(1)} %copy-done, bf16[1280,4096]{1,0:T(8,128)(2,1)} %all-gather.5.cloned.1.call-done, bf16[1,4096,344]{1,2,0:T(8,128)(2,1)} %param.18, f32[1280,344]{0,1:T(8,128)} %fusion.6), kind=kOutput, calls=%fused_computation | convolution fusion | flops 7222087680 | bytes 28368896 | tf_op jit(solution)/shard_map/dot_general | solution.py:132
  245.1 165.2 %reduce-scatter.2.cloned.1.call-done = bf16[40,4096]{1,0:T(8,128)(2,1)} async-done(((bf16[1280,4096]{1,0:T(8,128)(2,1)}), bf16[40,4096]{1,0:T(8,128)(2,1)}) %reduce-scatter.2.cloned.1.call-update) | async-done | bytes 327696 | tf_op jit(solution)/shard_map/reduce_scatter | solution.py:131
  410.3 1.7 copy.82
  412.0 5.3 %all-to-all-start.2 = ((bf16[40,8,512]{2,0,1:T(8,128)(2,1)}), bf16[40,8,512]{2,0,1:T(8,128)(2,1)S(1)}, u32[]{:S(2)}, u32[]{:S(2)}) async-start(bf16[40,8,512]{2,0,1:T(8,128)(2,1)} %bitcast.113), calls=%async_computation.3 | async-start | bytes 655360 | tf_op jit(solution)/shard_map/all_to_all | solution.py:137
  417.3 9.5 %all-to-all-done.2 = bf16[40,8,512]{2,0,1:T(8,128)(2,1)S(1)} async-done(((bf16[40,8,512]{2,0,1:T(8,128)(2,1)}), bf16[40,8,512]{2,0,1:T(8,128)(2,1)S(1)}, u32[]{:S(2)}, u32[]{:S(2)}) %all-to-all-start.2) | async-done | bytes 327712 | tf_op jit(solution)/shard_map/all_to_all | solution.py:137
  426.8 0.3 fusion.35
  427.2 0.8 fusion.40
  (34 shorter events, 0.9 us)
Async XLA Ops:
  6.5 219.2 %copy-start = (bf16[1,344,4096]{2,1,0:T(8,128)(2,1)S(1)}, bf16[1,344,4096]{2,1,0:T(8,128)(2,1)}, u32[]{:S(2)}) copy-start(bf16[1,344,4096]{2,1,0:T(8,128)(2,1)} %param.19) | copy-start | bytes 8454148
  6.5 76.1 %all-gather.3.cloned.1.call-start = ((), (), s32[]{:S(2)}) async-start(), calls=%async_computation.4 | async-start | bytes 4325376 | tf_op jit(solution)/shard_map/all_gather | solution.py:16
  9.7 75.7 %copy-start.3 = (bf16[128,256]{1,0:T(8,128)(2,1)S(1)}, bf16[128,256]{1,0:T(8,128)(2,1)}, u32[]{:S(2)}) copy-start(bf16[128,256]{1,0:T(8,128)(2,1)} %param.12) | copy-start | bytes 196612
  87.5 1.6 copy-start.1
  89.6 10.2 %copy-start.5 = (s32[128,2]{0,1:T(2,128)S(1)}, s32[128,2]{0,1:T(2,128)}, u32[]{:S(2)}) copy-start(s32[128,2]{0,1:T(2,128)} %param.20) | copy-start | bytes 3076
  89.6 31.4 %copy-start.2 = (bf16[128,512]{1,0:T(8,128)(2,1)S(1)}, bf16[128,512]{1,0:T(8,128)(2,1)}, u32[]{:S(2)}) copy-start(bf16[128,512]{1,0:T(8,128)(2,1)} %param.11) | copy-start | bytes 393220
  90.8 28.9 %all-to-all-start = ((bf16[8,512,128]{1,2,0:T(8,128)(2,1)}), bf16[8,512,128]{1,2,0:T(8,128)(2,1)}, u32[]{:S(2)}, u32[]{:S(2)}) async-start(bf16[8,512,128]{1,2,0:T(8,128)(2,1)} %bitcast.108), calls=%async_computation | async-start | bytes 2097152 | tf_op jit(solution)/shard_map/all_to_all | solution.py:28
  99.8 116.1 %all-gather.5.cloned.1.call-start = ((), (), s32[]{:S(2)}) async-start(), calls=%async_computation.5 | async-start | bytes 10813440 | tf_op jit(solution)/shard_map/all_gather | solution.py:127
  101.0 43.5 %copy-start.4 = (f32[4096]{0:T(1024)S(1)}, f32[4096]{0:T(1024)}, u32[]{:S(2)}) copy-start(f32[4096]{0:T(1024)} %param.16) | copy-start | bytes 49156
  145.4 264.9 %reduce-scatter.2.cloned.1.call-start = ((), (), s32[]{:S(2)}) async-start(), calls=%async_computation.6 | async-start | bytes 10813440 | tf_op jit(solution)/shard_map/reduce_scatter | solution.py:131
  245.0 172.3 %copy-start.6 = (f32[128,2]{0,1:T(2,128)S(1)}, f32[128,2]{0,1:T(2,128)}, u32[]{:S(2)}) copy-start(f32[128,2]{0,1:T(2,128)} %param.21) | copy-start | bytes 3076
  412.0 14.8 %all-to-all-start.2 = ((bf16[40,8,512]{2,0,1:T(8,128)(2,1)}), bf16[40,8,512]{2,0,1:T(8,128)(2,1)S(1)}, u32[]{:S(2)}, u32[]{:S(2)}) async-start(bf16[40,8,512]{2,0,1:T(8,128)(2,1)} %bitcast.113), calls=%async_computation.3 | async-start | bytes 655360 | tf_op jit(solution)/shard_map/all_to_all | solution.py:137
Sparse Core Ops, SparseCore 0:
  9.4 73.1 all-gather.2
  145.5 70.3 all-gather.4
  245.2 165.0 reduce-scatter.1
where the time goes:
time: 435 us; the launch traced here: 434 us
  waiting for transfers between devices  336 us (77%)
  matrix products  33 us (8%)
  blocking collectives  22.9 us (5%)
  starting transfers between devices  14.6 us (3%)
  between operations  13.3 us (3%)
  local copies, waits for them, and re-layouts  8.65 us (2%)
  other arithmetic  5.95 us (1%)
    reduce_scatter x1, waiting for transfers between devices, local(): lax.psum_scatter(jnp.dot(hidden, w_down, preferred_element_type=jnp.float...  165 us
    all_gather x1, waiting for transfers between devices, sent_together(): filled = lax.all_gather(both, axis, axis=dim, tiled=True)  72.9 us
    all_gather x1, waiting for transfers between devices, local(): piece_rows = lax.all_gather(arrived, 'ctx', axis=0, tiled=True)  70.3 us
    all_to_all x1, blocking collectives, local(): lax.all_to_all(buffer, 'exp', split_axis=0, concat_axis=1, tiled=True)  22.9 us
    dot_general x1, matrix products, local(): jnp.dot(hidden, w_down, preferred_element_type=jnp.float32)  19.3 us
    all_to_all x1, waiting for transfers between devices, summed_on_arrival(): lax.all_to_all(pieces, axis, split_axis=0, concat_axis=0, tiled=True)  18.2 us
    dot_general x1, matrix products, local(): gate_act = jnp.dot(piece_rows, w_gate, preferred_element_type=jnp.float32)  9.85 us
    all_to_all x1, waiting for transfers between devices, local(): lax.all_to_all(result, 'exp', split_axis=1, concat_axis=0, tiled=True)  9.49 us
  transfers between devices with their start and end apart: 5, of which 5 were waited for; matrix products, arithmetic and copies ran while one was open for 0% of the time, Pallas kernels for 0%

commit v1 on v0

v1 whole, which is shorter than its diff:
```python
import functools

import jax
import jax.numpy as jnp
from jax import lax
from jax.experimental import pallas as pl
from jax.experimental.pallas import tpu as pltpu
from jax.sharding import Mesh
from jax.sharding import PartitionSpec as P

HEAD_DIM = 128
EPSILON = 1e-05
MASKED = -1e30

AXES = ("zlo", "x", "core", "zhi", "y")
CTX = ("zlo", "x", "core")
RING = ("zlo", "x")
EXP = ("zhi", "y")
SWAP = [(0, 1), (1, 0)]

NT = (((1,), (1,)), ((), ()))


def attention_kernel(
    block_ref, query_ref, kv_ref, out_ref, max_ref, sum_ref, acc_ref, *, heads, chunk
):
    step = pl.program_id(0)
    rows = query_ref.shape[0]
    start = block_ref[0] * rows

    @pl.when(step == 0)
    def _():
        max_ref[...] = jnp.full_like(max_ref, MASKED)
        sum_ref[...] = jnp.zeros_like(sum_ref)
        acc_ref[...] = jnp.zeros_like(acc_ref)

    @pl.when(step * chunk < start + rows)
    def _():
        query_pos = start + lax.broadcasted_iota(jnp.int32, (rows, chunk), 0)
        key_pos = step * chunk + lax.broadcasted_iota(jnp.int32, (rows, chunk), 1)
        visible = key_pos <= query_pos
        for h in range(heads):
            cols = slice(h * HEAD_DIM, (h + 1) * HEAD_DIM)
            value_cols = slice((heads + h) * HEAD_DIM, (heads + h + 1) * HEAD_DIM)
            scores = lax.dot_general(
                query_ref[:, cols], kv_ref[:, cols], NT, preferred_element_type=jnp.float32
            ) * HEAD_DIM ** (-0.5)
            scores = jnp.where(visible, scores, MASKED)
            old_max = max_ref[h]
            new_max = jnp.maximum(old_max, jnp.max(scores, axis=1, keepdims=True))
            weights = jnp.where(visible, jnp.exp(scores - new_max[:, :1]), 0.0)
            rescale = jnp.exp(old_max - new_max)
            max_ref[h] = new_max
            sum_ref[h] = sum_ref[h] * rescale + jnp.sum(weights, axis=1, keepdims=True)
            acc_ref[h] = acc_ref[h] * rescale + jnp.dot(
                weights.astype(jnp.bfloat16),
                kv_ref[:, value_cols],
                preferred_element_type=jnp.float32,
            )

    @pl.when(step == pl.num_programs(0) - 1)
    def _():
        for h in range(heads):
            out_ref[:, h * HEAD_DIM : (h + 1) * HEAD_DIM] = (acc_ref[h] / sum_ref[h]).astype(
                out_ref.dtype
            )


def attention(block, query, kv, chunk=512):
    rows, width = query.shape
    heads = width // HEAD_DIM
    keys = kv.shape[0]

    def kv_index(step, block_ref):
        return (jnp.minimum(step, ((block_ref[0] + 1) * rows - 1) // chunk), 0)

    return pl.pallas_call(
        functools.partial(attention_kernel, heads=heads, chunk=chunk),
        grid_spec=pltpu.PrefetchScalarGridSpec(
            num_scalar_prefetch=1,
            grid=(keys // chunk,),
            in_specs=[
                pl.BlockSpec((rows, width), lambda step, block_ref: (0, 0)),
                pl.BlockSpec((chunk, 2 * width), kv_index),
            ],
            out_specs=pl.BlockSpec((rows, width), lambda step, block_ref: (0, 0)),
            scratch_shapes=[
                pltpu.VMEM((heads, rows, HEAD_DIM), jnp.float32),
                pltpu.VMEM((heads, rows, HEAD_DIM), jnp.float32),
                pltpu.VMEM((heads, rows, HEAD_DIM), jnp.float32),
            ],
        ),
        out_shape=jax.ShapeDtypeStruct((rows, width), jnp.bfloat16),
        cost_estimate=pl.CostEstimate(
            flops=4 * rows * width * keys,
            bytes_accessed=4 * keys * width,
            transcendentals=heads * rows * keys,
        ),
    )(block, query, kv)


def local(
    hidden_in,
    query_vectors,
    key_vectors,
    value_vectors,
    out_weight,
    norm_gain,
    gate_proj,
    up_proj,
    down_proj,
    expert_ids,
    gate_scale,
):
    row_count, local_width = hidden_in.shape
    model_width = out_weight.shape[1]
    expert_count = lax.axis_size(EXP)
    capacity = min(row_count, 5 * row_count // (2 * expert_count))

    kv = lax.all_gather(
        jnp.concatenate([key_vectors, value_vectors], axis=1), CTX, axis=0, tiled=True
    )

    def doubled(own):
        other = lax.ppermute(own, "core", SWAP)
        pad = jnp.zeros((-2 * own.shape[0] % 256, own.shape[1]), own.dtype)
        return jnp.concatenate([own, other, pad], axis=0)

    w_in = jnp.concatenate([doubled(gate_proj[0].T), doubled(up_proj[0].T)], axis=0)
    w_down = doubled(down_proj[0])
    units = w_down.shape[0]

    flat_ids = expert_ids.reshape(row_count * 2)
    onehot = (
        flat_ids[:, None] == lax.broadcasted_iota(jnp.int32, (row_count * 2, expert_count), 1)
    ).astype(jnp.int32)
    earlier = jnp.cumsum(onehot, axis=0) - onehot
    slot_index = jnp.sum(earlier * onehot, axis=1)
    target = flat_ids * capacity + slot_index
    placing = (
        target[None, :]
        == lax.broadcasted_iota(jnp.int32, (expert_count * capacity, row_count * 2), 0)
    ).astype(jnp.bfloat16)
    placing_tokens = jnp.sum(placing.reshape(expert_count * capacity, row_count, 2), axis=2)

    w_out = lax.all_to_all(out_weight, EXP, split_axis=1, concat_axis=0, tiled=True)

    block = lax.axis_index(CTX).reshape(1)
    attended = attention(block, query_vectors, kv)
    all_heads = lax.all_gather(attended, EXP, axis=1, tiled=True)
    projected = jnp.dot(all_heads, w_out, preferred_element_type=jnp.float32)
    residual = (hidden_in.astype(jnp.float32) + projected).astype(jnp.bfloat16)
    residual_wide = residual.astype(jnp.float32)

    buffer = jnp.dot(placing_tokens, residual, preferred_element_type=jnp.float32).astype(
        jnp.bfloat16
    )
    arrived = lax.all_to_all(buffer, EXP, split_axis=0, concat_axis=1, tiled=True)
    arrived_wide = arrived.astype(jnp.float32)
    inverse = lax.rsqrt(jnp.mean(arrived_wide * arrived_wide, axis=1, keepdims=True) + EPSILON)
    normed = (arrived_wide * inverse * norm_gain[None, :]).astype(jnp.bfloat16)

    rows = lax.all_gather(normed, RING, axis=0, tiled=True)
    act = lax.dot_general(rows, w_in, NT, preferred_element_type=jnp.float32)
    hidden = (jax.nn.silu(act[:, :units]) * act[:, units:]).astype(jnp.bfloat16)
    result = lax.psum_scatter(
        jnp.dot(hidden, w_down, preferred_element_type=jnp.float32).astype(jnp.bfloat16),
        RING,
        scatter_dimension=0,
        tiled=True,
    )
    returned = lax.all_to_all(result, EXP, split_axis=1, concat_axis=0, tiled=True)
    gathered_back = lax.dot_general(
        placing, returned, (((0,), (0,)), ((), ())), preferred_element_type=jnp.float32
    )
    gathered_back = gathered_back.reshape(row_count, 2, local_width)
    combined = (
        residual_wide
        + gate_scale[:, 0:1] * gathered_back[:, 0]
        + gate_scale[:, 1:2] * gathered_back[:, 1]
    )
    return combined.astype(jnp.bfloat16)


def solution(mesh):
    fine = Mesh(mesh.devices.reshape(4, 4, 2, 2, 4), AXES)
    placed = (
        P(CTX, EXP),
        P(CTX, EXP),
        P(CTX, EXP),
        P(CTX, EXP),
        P(EXP, None),
        P(),
        P(EXP, None, CTX),
        P(EXP, None, CTX),
        P(EXP, CTX, None),
        P(CTX, None),
        P(CTX, None),
    )
    return jax.shard_map(
        local, mesh=fine, in_specs=placed, out_specs=P(CTX, EXP), check_vma=False
    )
```

time: 435 us -> 423 us (0.972)
  waiting for transfers between devices: 336 us -> 276 us
  blocking collectives: 22.9 us -> 64.9 us
  matrix products: 33 us -> 22.5 us
  local copies, waits for them, and re-layouts: 8.65 us -> 17.9 us
  starting transfers between devices: 14.6 us -> 20.2 us
    reduce_scatter x1, waiting for transfers between devices: 165 us -> 95.7 us  [local(): lax.psum_scatter(jnp.dot(hidden, w_down, preferred_element_type=jnp.float...]
    all_gather x0 -> x1, blocking collectives: none -> 45.6 us  [local(): all_heads = lax.all_gather(attended, EXP, axis=1, tiled=True)]
    all_to_all x2, waiting for transfers between devices: 27.7 us -> 56.1 us  [the longest x1 46.6 us: local(): lax.all_to_all(out_weight, EXP, split_axis=1, concat_axis=0, tiled=True)]
    all_gather x2, waiting for transfers between devices: 143 us -> 121 us  [the longest x1 80 us: local(): rows = lax.all_gather(normed, RING, axis=0, tiled=True)]
    dot_general x1, matrix products: 19.3 us -> 7.41 us  [local(): jnp.dot(hidden, w_down, preferred_element_type=jnp.float32)]
    unnamed x17 -> x21, local copies, waits for them, and re-layouts: 2.34 us -> 12.2 us
    all_to_all x2, starting transfers between devices: 14.3 us -> 19.4 us  [the longest x1 11.5 us: local(): lax.all_to_all(out_weight, EXP, split_axis=1, concat_axis=0, tiled=True)]
    dot_general x4 -> x2, matrix products: 13.1 us -> 14.6 us  [the longest x1 12.5 us: local(): act = lax.dot_general(rows, w_in, NT, preferred_element_type=jnp.float32)]
  transfers between devices with their start and end apart: 5 -> 8, of which waited for: 5 -> 6; matrix products, arithmetic and copies ran while one was open for 0% -> 7% of each run, Pallas kernels for 0% -> 0%
where the time goes in v1:
time: 423 us; the launch traced here: 422 us
  waiting for transfers between devices  276 us (65%)
  blocking collectives  64.9 us (15%)
  matrix products  22.5 us (5%)
  starting transfers between devices  20.2 us (5%)
  local copies, waits for them, and re-layouts  17.9 us (4%)
  between operations  13.3 us (3%)
  other arithmetic  4.23 us (1%)
    reduce_scatter x1, waiting for transfers between devices, local(): lax.psum_scatter(jnp.dot(hidden, w_down, preferred_element_type=jnp.float...  95.7 us
    all_gather x1, waiting for transfers between devices, local(): rows = lax.all_gather(normed, RING, axis=0, tiled=True)  80 us
    all_to_all x1, waiting for transfers between devices, local(): lax.all_to_all(out_weight, EXP, split_axis=1, concat_axis=0, tiled=True)  46.6 us
    all_gather x1, blocking collectives, local(): all_heads = lax.all_gather(attended, EXP, axis=1, tiled=True)  45.6 us
    all_gather x1, waiting for transfers between devices, local(): lax.all_gather(jnp.concatenate([key_vectors, value_vectors], axis=1), CTX...  41.4 us
    all_to_all x1, blocking collectives, local(): lax.all_to_all(buffer, EXP, split_axis=0, concat_axis=1, tiled=True)  19.3 us
    dot_general x1, matrix products, local(): act = lax.dot_general(rows, w_in, NT, preferred_element_type=jnp.float32)  12.5 us
    unnamed x21, local copies, waits for them, and re-layouts  12.2 us
  transfers between devices with their start and end apart: 8, of which 6 were waited for; matrix products, arithmetic and copies ran while one was open for 7% of the time, Pallas kernels for 0%

profile of v1, /device:TPU:8, one launch (start us, length us, event | category | flops | bytes accessed | tf_op | source)
XLA Modules:
  0.0 422.0 jit_solution(2573593733493698144)
XLA Ops:
  6.5 1.5 pad_maximum_fusion
  8.1 4.1 copy.49
  12.2 11.5 %all-to-all-start = ((bf16[256,8,512]{0,2,1:T(8,128)(2,1)}), bf16[256,8,512]{0,2,1:T(8,128)(2,1)S(1)}, u32[]{:S(2)}, u32[]{:S(2)}) async-start(bf16[256,8,512]{0,2,1:T(8,128)(2,1)} %bitcast.66), calls=%async_computation | async-start | bytes 4194304 | tf_op jit(solution)/shard_map/all_to_all | solution.py:146
  24.2 0.6 reduce-window.6
  24.7 0.2 slice_reduce_fusion
  25.4 46.6 %all-to-all-done = bf16[256,8,512]{0,2,1:T(8,128)(2,1)S(1)} async-done(((bf16[256,8,512]{0,2,1:T(8,128)(2,1)}), bf16[256,8,512]{0,2,1:T(8,128)(2,1)S(1)}, u32[]{:S(2)}, u32[]{:S(2)}) %all-to-all-start) | async-done | bytes 2097184 | tf_op jit(solution)/shard_map/all_to_all | solution.py:146
  72.0 2.4 copy.50
  74.3 41.4 %all-gather.3.cloned.1.call-done.kv_ref = bf16[4096,512]{1,0:T(8,128)(2,1)} async-done(((bf16[128,512]{1,0:T(8,128)(2,1)}), bf16[4096,512]{1,0:T(8,128)(2,1)}) %all-gather.3.cloned.1.call-update) | async-done | bytes 4194320 | tf_op jit(solution)/shard_map/all_gather | solution.py:120
  115.7 2.9 shard_map.109
  118.6 45.6 %all_gather.10 = bf16[128,2048]{1,0:T(8,128)(2,1)S(1)} all-gather(bf16[128,256]{1,0:T(8,128)(2,1)} %shard_map.109), channel_id=1, replica_groups=mesh['zlo'=4,'x'=4,'core'=2,'zhi'=2,'y'=4] {'zhi','y'}, dimensions={1}, use_global_device_ids=true | all-gather | bytes 589824 | tf_op jit(solution)/shard_map/all_gather | solution.py:150
  164.2 2.0 fusion.6
  166.3 0.2 convolution_convert_fusion.1
  166.5 19.3 %all_to_all.51 = bf16[8,40,512]{2,1,0:T(8,128)(2,1)S(1)} all-to-all(bf16[8,40,512]{2,1,0:T(8,128)(2,1)S(1)} %bitcast.72), channel_id=1, replica_groups=mesh['zlo'=4,'x'=4,'core'=2,'zhi'=2,'y'=4] {'zhi','y'}, dimensions={0} | all-to-all | bytes 655360 | tf_op jit(solution)/shard_map/all_to_all | solution.py:158
  185.9 0.2 fusion.9
  186.1 0.9 multiply_convert_fusion
  187.2 0.5 collective-permute-start.1
  187.8 1.7 constant_dynamic-update-slice_fusion.3
  189.5 2.8 collective-permute-done
  192.4 1.8 constant_dynamic-update-slice_fusion.2
  194.2 0.9 broadcast_dynamic-update-slice_fusion
  195.1 1.8 constant_dynamic-update-slice_fusion.1
  196.9 1.7 constant_dynamic-update-slice_fusion
  198.6 0.9 broadcast_dynamic-update-slice_fusion.1
  199.5 80.0 %all-gather.5.cloned.1.call-done = bf16[640,4096]{1,0:T(8,128)(2,1)} async-done(((bf16[40,4096]{1,0:T(8,128)(2,1)}), bf16[640,4096]{1,0:T(8,128)(2,1)}) %all-gather.5.cloned.1.call-update) | async-done | bytes 5242896 | tf_op jit(solution)/shard_map/all_gather | solution.py:163
  279.5 12.5 %fusion.26 = f32[640,1536]{1,0:T(8,128)S(1)} fusion(bf16[640,4096]{1,0:T(8,128)(2,1)} %all-gather.5.cloned.1.call-done, bf16[1536,4096]{1,0:T(8,128)(2,1)} %broadcast_dynamic-update-slice_fusion.1), kind=kOutput, calls=%fused_computation.51 | convolution fusion | flops 8053063680 | bytes 21757952 | tf_op jit(solution)/shard_map/dot_general | solution.py:164
  292.1 7.4 %convolution_convert_fusion = bf16[640,4096]{1,0:T(8,128)(2,1)} fusion(bf16[80,4096]{1,0:T(8,128)(2,1)S(1)} %broadcast.49, bf16[344,4096]{1,0:T(8,128)(2,1)} %collective-permute-done.2, bf16[344,4096]{1,0:T(8,128)(2,1)S(1)} %bitcast.75, f32[640,1536]{1,0:T(8,128)S(1)} %fusion.26), kind=kOutput, calls=%fused_computation | convolution fusion | flops 4050976768 | bytes 15466496 | tf_op jit(solution)/shard_map/dot_general | solution.py:167
  299.5 95.7 %reduce-scatter.2.cloned.1.call-done = bf16[40,4096]{1,0:T(8,128)(2,1)} async-done(((bf16[640,4096]{1,0:T(8,128)(2,1)}), bf16[40,4096]{1,0:T(8,128)(2,1)}) %reduce-scatter.2.cloned.1.call-update) | async-done | bytes 327696 | tf_op jit(solution)/shard_map/reduce_scatter | solution.py:166
  395.2 1.7 copy.59
  397.0 7.9 %all-to-all-start.2 = ((bf16[40,8,512]{2,0,1:T(8,128)(2,1)}), bf16[40,8,512]{2,0,1:T(8,128)(2,1)S(1)}, u32[]{:S(2)}, u32[]{:S(2)}) async-start(bf16[40,8,512]{2,0,1:T(8,128)(2,1)} %bitcast.64), calls=%async_computation.3 | async-start | bytes 655360 | tf_op jit(solution)/shard_map/all_to_all | solution.py:172
  404.9 9.5 %all-to-all-done.2 = bf16[40,8,512]{2,0,1:T(8,128)(2,1)S(1)} async-done(((bf16[40,8,512]{2,0,1:T(8,128)(2,1)}), bf16[40,8,512]{2,0,1:T(8,128)(2,1)S(1)}, u32[]{:S(2)}, u32[]{:S(2)}) %all-to-all-start.2) | async-done | bytes 327712 | tf_op jit(solution)/shard_map/all_to_all | solution.py:172
  414.4 0.3 fusion.11
  414.7 0.8 fusion.16
  (40 shorter events, 1.3 us)
Async XLA Ops:
  6.5 17.2 %copy-start.4 = (s32[128,2]{0,1:T(2,128)S(1)}, s32[128,2]{0,1:T(2,128)}, u32[]{:S(2)}) copy-start(s32[128,2]{0,1:T(2,128)} %param.20) | copy-start | bytes 3076
  6.5 109.2 %all-gather.3.cloned.1.call-start = ((), (), s32[]{:S(2)}) async-start(), calls=%async_computation.4 | async-start | bytes 4325376 | tf_op jit(solution)/shard_map/all_gather | solution.py:120
  12.2 59.8 %all-to-all-start = ((bf16[256,8,512]{0,2,1:T(8,128)(2,1)}), bf16[256,8,512]{0,2,1:T(8,128)(2,1)S(1)}, u32[]{:S(2)}, u32[]{:S(2)}) async-start(bf16[256,8,512]{0,2,1:T(8,128)(2,1)} %bitcast.66), calls=%async_computation | async-start | bytes 4194304 | tf_op jit(solution)/shard_map/all_to_all | solution.py:146
  23.7 140.5 %copy-start.2 = (bf16[128,512]{1,0:T(8,128)(2,1)S(1)}, bf16[128,512]{1,0:T(8,128)(2,1)}, u32[]{:S(2)}) copy-start(bf16[128,512]{1,0:T(8,128)(2,1)} %param.11) | copy-start | bytes 393220
  23.7 255.8 %all-gather.5.cloned.1.call-start = ((), (), s32[]{:S(2)}) async-start(), calls=%async_computation.5 | async-start | bytes 5570560 | tf_op jit(solution)/shard_map/all_gather | solution.py:163
  115.7 70.4 %copy-start.3 = (f32[4096]{0:T(1024)S(1)}, f32[4096]{0:T(1024)}, u32[]{:S(2)}) copy-start(f32[4096]{0:T(1024)} %param.16) | copy-start | bytes 49156
  118.6 68.5 %copy-start = (bf16[1,4096,344]{1,2,0:T(8,128)(2,1)S(1)}, bf16[1,4096,344]{1,2,0:T(8,128)(2,1)}, u32[]{:S(2)}) copy-start(bf16[1,4096,344]{1,2,0:T(8,128)(2,1)} %param.17) | copy-start | bytes 8454148
  187.0 208.2 %reduce-scatter.2.cloned.1.call-start = ((), (), s32[]{:S(2)}) async-start(), calls=%async_computation.6 | async-start | bytes 5570560 | tf_op jit(solution)/shard_map/reduce_scatter | solution.py:166
  187.1 5.3 %collective-permute-start = (bf16[344,4096]{1,0:T(8,128)(2,1)S(1)}, bf16[344,4096]{1,0:T(8,128)(2,1)S(1)}, u32[]{:S(2)}, u32[]{:S(2)}) collective-permute-start(bf16[344,4096]{1,0:T(8,128)(2,1)S(1)} %bitcast.68), channel_id=1, source_target_pairs={{0,8},{8,0},{1,9},{9,1},{2,10},{10,2},{3,11},{11,3},{4,12},{12,4},... | collective-permute-start | bytes 8454152 | tf_op jit(solution)/shard_map/ppermute | solution.py:125
  187.2 9.7 %collective-permute-start.1 = (bf16[344,4096]{1,0:T(8,128)(2,1)}, bf16[344,4096]{1,0:T(8,128)(2,1)S(1)}, u32[]{:S(2)}, u32[]{:S(2)}) collective-permute-start(bf16[344,4096]{1,0:T(8,128)(2,1)} %bitcast.69), channel_id=1, source_target_pairs={{0,8},{8,0},{1,9},{9,1},{2,10},{10,2},{3,11},{11,3},{4,12},{12,4},... | collective-permute-start | bytes 8454152 | tf_op jit(solution)/shard_map/ppermute | solution.py:125
  187.7 7.4 %copy-start.1 = (bf16[1,4096,344]{1,2,0:T(8,128)(2,1)S(1)}, bf16[1,4096,344]{1,2,0:T(8,128)(2,1)}, u32[]{:S(2)}) copy-start(bf16[1,4096,344]{1,2,0:T(8,128)(2,1)} %param.18) | copy-start | bytes 8454148
  187.7 104.4 %collective-permute-start.2 = (bf16[344,4096]{1,0:T(8,128)(2,1)}, bf16[344,4096]{1,0:T(8,128)(2,1)}, u32[]{:S(2)}, u32[]{:S(2)}) collective-permute-start(bf16[344,4096]{1,0:T(8,128)(2,1)} %bitcast.74), channel_id=1, source_target_pairs={{0,8},{8,0},{1,9},{9,1},{2,10},{10,2},{3,11},{11,3},{4,12},{12,4},... | collective-permute-start | bytes 8454152 | tf_op jit(solution)/shard_map/ppermute | solution.py:125
  199.5 92.6 %copy-start.6 = (bf16[1,344,4096]{2,1,0:T(8,128)(2,1)S(1)}, bf16[1,344,4096]{2,1,0:T(8,128)(2,1)}, u32[]{:S(2)}) copy-start(bf16[1,344,4096]{2,1,0:T(8,128)(2,1)} %param.19) | copy-start | bytes 8454148
  299.5 105.3 %copy-start.5 = (f32[128,2]{0,1:T(2,128)S(1)}, f32[128,2]{0,1:T(2,128)}, u32[]{:S(2)}) copy-start(f32[128,2]{0,1:T(2,128)} %param.21) | copy-start | bytes 3076
  397.0 17.4 %all-to-all-start.2 = ((bf16[40,8,512]{2,0,1:T(8,128)(2,1)}), bf16[40,8,512]{2,0,1:T(8,128)(2,1)S(1)}, u32[]{:S(2)}, u32[]{:S(2)}) async-start(bf16[40,8,512]{2,0,1:T(8,128)(2,1)} %bitcast.64), calls=%async_computation.3 | async-start | bytes 655360 | tf_op jit(solution)/shard_map/all_to_all | solution.py:172
Sparse Core Ops, SparseCore 0:
  9.2 106.4 all-gather.2
  187.1 92.3 all-gather.4
  299.7 95.5 reduce-scatter.1
